TPU v7x, 1024 devices: a whole 4x8x16 slice. The times are simulated.
1024 devices in a mesh: dp: 128 (over x, z, y_hi), tensor: 8 (over y_lo, core).
Axes of the slice: x: 4, y: 8 (y_hi: 2, y_lo: 4; y = y_hi * 4 + y_lo), z: 16, core: 2. Of those that a mesh axis runs over, the one named last changes fastest.
Arguments:
- residual: bfloat16 [2, 8192, 5120], P(None, 'dp'), may hold values from -6 to 6
- context: bfloat16 [2, 8192, 3072], P(None, 'dp', 'tensor'), may hold values from -24 to 24
- w_out: bfloat16 [3072, 5120], P('tensor'), may hold values from -0.109375 to 0.109375
- gain: float32 [5120], replicated, may hold values from 0.1 to 1.9
- cotangent: bfloat16 [2, 8192, 5120], P(None, 'dp'), may hold values from -6 to 6
- slot_rows: int32 [8, 32], P('tensor'), may hold values from 0 to 383, as said below
Outputs:
- grad_slots: float32 [8, 5120, 32], P('tensor', 'dp')
- ctx_grad: bfloat16 [2, 8192, 3072], P(None, 'dp', 'tensor')
- resid_grad: bfloat16 [2, 8192, 5120], P(None, 'dp')
Inputs may be any that keep to these rules, and one draw needn't show every extreme that they name: Each row of slot_rows holds 32 different numbers.
All inputs are finite; a program needn't handle non-finite values.
Results may differ from a plain program's by a relative error of at most 0.006.
Values may be sent and summed in bfloat16 or wider, within the bound.
No kernel may reach another device: no remote copies, remote signals or barrier semaphores. Data moves between devices by JAX's collectives and lax.ppermute only.
A program may use at most 64 MiB of HBM per device.

v0:
```python
import jax
import jax.numpy as jnp
from jax import lax
from jax.sharding import Mesh
from jax.sharding import PartitionSpec as P

DP = ("dp_0", "dp_1", "dp_2")


def in_blocks(array, dim, length):
    before, after = (array.shape[:dim], array.shape[dim + 1 :])
    return jnp.moveaxis(array.reshape(*before, length, -1, *after), dim, 0)


def sent_and_summed(array, axis, dim):
    length = lax.axis_size(axis)
    parts = lax.all_to_all(in_blocks(array, dim, length), axis, 0, 0, tiled=True)
    return jnp.sum(parts.astype(jnp.float32), axis=0)


def sent_to_all(array, axis):
    length = lax.axis_size(axis)
    return lax.all_to_all(
        jnp.broadcast_to(array[None], (length, *array.shape)), axis, 0, 0, tiled=True
    )


def joined_along(parts, dim):
    dims = list(parts.shape[1:])
    dims[dim] *= parts.shape[0]
    return jnp.moveaxis(parts, 0, dim).reshape(dims)


def gathered_copies(array, axis, dim):
    parts = sent_to_all(array, axis)
    return joined_along(parts, dim)


def scatter_axes(array, axes, dim):
    for axis in axes:
        array = lax.psum_scatter(array, axis, scatter_dimension=dim, tiled=True)
    return array


def norm_backward(res_rows, summed, gain, cot_rows):
    hidden = res_rows.astype(jnp.float32) + summed
    center = hidden - jnp.mean(hidden, axis=-1, keepdims=True)
    inverse = lax.rsqrt(jnp.mean(center * center, axis=-1, keepdims=True) + 1e-05)
    normed = center * inverse
    upstream = cot_rows.astype(jnp.float32) * gain
    result = inverse * (
        upstream
        - jnp.mean(upstream, axis=-1, keepdims=True)
        - normed * jnp.mean(upstream * normed, axis=-1, keepdims=True)
    )
    return result.astype(jnp.bfloat16)


def weight_term(grad_rows, columns):
    return lax.dot_general(
        grad_rows, columns, (((0,), (0,)), ((), ())), preferred_element_type=jnp.float32
    )


def body(residual, context, w_out, gain, cotangent, slot_rows):
    micro_count = residual.shape[0]
    order = slot_rows[0]
    resid_list = []
    ctx_list = []
    for micro_idx in range(micro_count):
        partial_value = jnp.dot(context[micro_idx], w_out, preferred_element_type=jnp.float32)
        share = sent_and_summed(partial_value.astype(jnp.bfloat16), "tensor", 0)
        share_rows = share.shape[0]
        first_row = lax.axis_index("tensor") * share_rows
        res_share = lax.dynamic_slice_in_dim(residual[micro_idx], first_row, share_rows, 0)
        cot_share = lax.dynamic_slice_in_dim(cotangent[micro_idx], first_row, share_rows, 0)
        grad_share = norm_backward(res_share, share, gain, cot_share)
        grad_rows = gathered_copies(grad_share, "tensor", 0)
        resid_list.append(grad_rows)
        ctx_back = lax.dot_general(
            grad_rows, w_out, (((1,), (1,)), ((), ())), preferred_element_type=jnp.float32
        )
        ctx_list.append(ctx_back.astype(jnp.bfloat16))
    replicas = lax.axis_size(DP)
    gradient = weight_term(resid_list[0], jnp.take(context[0], order, axis=1))
    micro_idx = 1
    gradient = gradient + weight_term(
        resid_list[micro_idx], jnp.take(context[micro_idx], order, axis=1)
    )
    reduced = scatter_axes(gradient, DP, 0)
    grad_slots = (reduced / replicas)[None]
    return (grad_slots, jnp.stack(ctx_list), jnp.stack(resid_list))


def solution(mesh):
    split = Mesh(
        mesh.devices.reshape(4, 16, 2, mesh.shape["tensor"]), ("dp_0", "dp_1", "dp_2", "tensor")
    )
    in_specs = (
        P(None, DP, None),
        P(None, DP, "tensor"),
        P("tensor", None),
        P(),
        P(None, DP, None),
        P("tensor", None),
    )
    out_specs = (P("tensor", DP, None), P(None, DP, "tensor"), P(None, DP, None))
    return jax.shard_map(body, mesh=split, in_specs=in_specs, out_specs=out_specs, check_vma=False)
```

profile of v0, /device:TPU:2, one launch (start us, length us, event | category | flops | bytes accessed | tf_op | source)
XLA Modules:
  0.0 244.2 jit_solution(16910082662995485897)
XLA Ops:
  7.2 0.0 copy-start.1
  7.2 3.8 %fusion = bf16[8,8,5120]{2,1,0:T(8,128)(2,1)} fusion(bf16[384,5120]{1,0:T(8,128)(2,1)} %param.10, bf16[2,64,384]{2,1,0:T(8,128)(2,1)} %param.9), kind=kOutput, calls=%fused_computation.4 | convolution fusion | flops 251985920 | bytes 4636672 | tf_op jit(solution)/shard_map/dot_general | solution.py:71
  11.0 4.9 %all-to-all-start = ((bf16[8,8,5120]{2,1,0:T(8,128)(2,1)}), bf16[8,8,5120]{2,1,0:T(8,128)(2,1)S(1)}, u32[]{:S(2)}, u32[]{:S(2)}) async-start(bf16[8,8,5120]{2,1,0:T(8,128)(2,1)} %fusion), calls=%async_computation | async-start | bytes 1310720 | tf_op jit(solution)/shard_map/all_to_all | solution.py:17
  15.9 0.0 copy-done.1
  15.9 0.0 copy-start
  15.9 3.9 %fusion.1 = bf16[8,8,5120]{2,1,0:T(8,128)(2,1)} fusion(bf16[384,5120]{1,0:T(8,128)(2,1)} %param.10, bf16[2,64,384]{2,1,0:T(8,128)(2,1)S(1)} %copy-done.1), kind=kOutput, calls=%fused_computation.5 | convolution fusion | flops 251985920 | bytes 4636672 | tf_op jit(solution)/shard_map/dot_general | solution.py:71
  19.8 0.0 copy-done
  19.8 0.1 fusion.53
  19.9 14.2 %all-to-all-done = bf16[8,8,5120]{2,1,0:T(8,128)(2,1)S(1)} async-done(((bf16[8,8,5120]{2,1,0:T(8,128)(2,1)}), bf16[8,8,5120]{2,1,0:T(8,128)(2,1)S(1)}, u32[]{:S(2)}, u32[]{:S(2)}) %all-to-all-start) | async-done | bytes 655392 | tf_op jit(solution)/shard_map/all_to_all | solution.py:17
  34.0 3.5 %all-to-all-start.2 = ((bf16[8,8,5120]{2,1,0:T(8,128)(2,1)}), bf16[8,8,5120]{2,1,0:T(8,128)(2,1)S(1)}, u32[]{:S(2)}, u32[]{:S(2)}) async-start(bf16[8,8,5120]{2,1,0:T(8,128)(2,1)} %fusion.1), calls=%async_computation.2 | async-start | bytes 1310720 | tf_op jit(solution)/shard_map/all_to_all | solution.py:17
  37.6 2.2 fusion.52
  39.8 0.1 convert_reduce_fusion.1
  39.9 0.0 copy-start.2
  39.9 0.2 fusion.38
  40.0 0.2 multiply_reduce_fusion.1
  40.3 15.3 %all-to-all-done.2 = bf16[8,8,5120]{2,1,0:T(8,128)(2,1)S(1)} async-done(((bf16[8,8,5120]{2,1,0:T(8,128)(2,1)}), bf16[8,8,5120]{2,1,0:T(8,128)(2,1)S(1)}, u32[]{:S(2)}, u32[]{:S(2)}) %all-to-all-start.2) | async-done | bytes 655392 | tf_op jit(solution)/shard_map/all_to_all | solution.py:17
  55.6 0.1 convert_reduce_fusion
  55.7 0.2 fusion.37
  55.9 0.2 multiply_reduce_fusion
  56.1 1.2 fusion.23
  57.3 1.1 fusion.33
  58.4 20.5 %all_to_all.20 = bf16[8,8,5120]{2,1,0:T(8,128)(2,1)S(1)} all-to-all(bf16[8,8,5120]{2,1,0:T(8,128)(2,1)S(1)} %broadcast_in_dim.17), channel_id=1, replica_groups=mesh['dp_0'=4,'dp_1'=16,'dp_2'=2,'tensor'=8] {'tensor'}, dimensions={0} | all-to-all | bytes 1310720 | tf_op jit(solution)/shard_map/all_to_all | solution.py:23
  79.0 0.9 broadcast_in_dim.19
  79.9 3.5 %all-to-all-start.3 = ((bf16[8,8,5120]{2,1,0:T(8,128)(2,1)}), bf16[8,8,5120]{2,1,0:T(8,128)(2,1)S(1)}, u32[]{:S(2)}, u32[]{:S(2)}) async-start(bf16[8,8,5120]{2,1,0:T(8,128)(2,1)} %broadcast_in_dim.19), calls=%async_computation.3 | async-start | bytes 1310720 | tf_op jit(solution)/shard_map/all_to_all | solution.py:23
  83.4 0.0 reduce-scatter.6.cloned.1.call-start
  83.5 0.1 copy.18
  83.6 0.1 copy.17
  83.7 0.0 copy-done.2
  83.8 0.6 gather_fusion.1
  84.4 0.6 gather_fusion
  85.0 0.3 fusion.7
  85.3 16.2 %all-to-all-done.3 = bf16[8,8,5120]{2,1,0:T(8,128)(2,1)S(1)} async-done(((bf16[8,8,5120]{2,1,0:T(8,128)(2,1)}), bf16[8,8,5120]{2,1,0:T(8,128)(2,1)S(1)}, u32[]{:S(2)}, u32[]{:S(2)}) %all-to-all-start.3) | async-done | bytes 655392 | tf_op jit(solution)/shard_map/all_to_all | solution.py:23
  101.5 1.1 convolution_add_fusion
  102.6 0.0 reduce-scatter.6.cloned.1.call-update
  102.6 0.0 reduce-scatter.8.cloned.1.call-start
  102.7 1.3 dynamic-slice.4
  104.6 3.4 %fusion.3 = bf16[1,64,384]{2,1,0:T(8,128)(2,1)S(1)} fusion(bf16[384,5120]{1,0:T(8,128)(2,1)} %param.10, bf16[8,8,5120]{2,1,0:T(8,128)(2,1)S(1)} %all-to-all-done.3), kind=kOutput, calls=%fused_computation.13 | convolution fusion | flops 251682816 | bytes 4636672 | tf_op jit(solution)/shard_map/dot_general | solution.py:80
  108.0 1.2 pad_maximum_fusion
  109.2 32.7 %reduce-scatter.6.cloned.1.call-done = f32[1280,32]{0,1:T(8,128)} async-done(((f32[5120,32]{0,1:T(8,128)}), f32[1280,32]{0,1:T(8,128)}) %reduce-scatter.6.cloned.1.call-update) | async-done | bytes 163856 | tf_op jit(solution)/shard_map/reduce_scatter | solution.py:41
  142.0 2.0 copy.13
  144.0 0.0 reduce-scatter.8.cloned.1.call-update
  144.0 3.4 %fusion.2 = bf16[1,64,384]{2,1,0:T(8,128)(2,1)S(1)} fusion(bf16[384,5120]{1,0:T(8,128)(2,1)} %param.10, bf16[8,8,5120]{2,1,0:T(8,128)(2,1)S(1)} %all_to_all.20), kind=kOutput, calls=%fused_computation.12 | convolution fusion | flops 251682816 | bytes 4636672 | tf_op jit(solution)/shard_map/dot_general | solution.py:80
  147.4 0.7 pad_maximum_fusion.1
  148.1 71.6 %reduce-scatter.8.cloned.1.call-done = f32[80,32]{1,0:T(8,128)} async-done(((f32[1280,32]{1,0:T(8,128)}), f32[80,32]{1,0:T(8,128)}) %reduce-scatter.8.cloned.1.call-update) | async-done | bytes 10256
  219.7 0.8 copy.14
  220.5 16.2 %all-reduce = f32[80,32]{0,1:T(8,128)S(1)} all-reduce(f32[80,32]{0,1:T(8,128)S(1)} %copy.14), channel_id=4, replica_groups=mesh['dp_0'=4,'dp_1'=16,'dp_2'=2,'tensor'=8] {'dp_2'}, use_global_device_ids=true, to_apply=%region_12.14.clone | all-reduce | flops 2560 | bytes 20480
  236.7 0.7 fusion.39
  (11 shorter events, 0.1 us)
Async XLA Ops:
  7.2 8.7 %copy-start.1 = (bf16[2,64,384]{2,1,0:T(8,128)(2,1)S(1)}, bf16[2,64,384]{2,1,0:T(8,128)(2,1)}, u32[]{:S(2)}) copy-start(bf16[2,64,384]{2,1,0:T(8,128)(2,1)} %param.9) | copy-start | bytes 294916
  11.0 23.0 %all-to-all-start = ((bf16[8,8,5120]{2,1,0:T(8,128)(2,1)}), bf16[8,8,5120]{2,1,0:T(8,128)(2,1)S(1)}, u32[]{:S(2)}, u32[]{:S(2)}) async-start(bf16[8,8,5120]{2,1,0:T(8,128)(2,1)} %fusion), calls=%async_computation | async-start | bytes 1310720 | tf_op jit(solution)/shard_map/all_to_all | solution.py:17
  15.9 3.9 %copy-start = (bf16[2,64,5120]{2,1,0:T(8,128)(2,1)S(1)}, bf16[2,64,5120]{2,1,0:T(8,128)(2,1)}, u32[]{:S(2)}) copy-start(bf16[2,64,5120]{2,1,0:T(8,128)(2,1)} %param.8) | copy-start | bytes 3932164
  34.0 21.6 %all-to-all-start.2 = ((bf16[8,8,5120]{2,1,0:T(8,128)(2,1)}), bf16[8,8,5120]{2,1,0:T(8,128)(2,1)S(1)}, u32[]{:S(2)}, u32[]{:S(2)}) async-start(bf16[8,8,5120]{2,1,0:T(8,128)(2,1)} %fusion.1), calls=%async_computation.2 | async-start | bytes 1310720 | tf_op jit(solution)/shard_map/all_to_all | solution.py:17
  39.9 43.9 %copy-start.2 = (s32[1,32]{1,0:T(1,128)S(1)}, s32[1,32]{1,0:T(1,128)}, u32[]{:S(2)}) copy-start(s32[1,32]{1,0:T(1,128)} %param.13) | copy-start | bytes 388
  79.9 21.6 %all-to-all-start.3 = ((bf16[8,8,5120]{2,1,0:T(8,128)(2,1)}), bf16[8,8,5120]{2,1,0:T(8,128)(2,1)S(1)}, u32[]{:S(2)}, u32[]{:S(2)}) async-start(bf16[8,8,5120]{2,1,0:T(8,128)(2,1)} %broadcast_in_dim.19), calls=%async_computation.3 | async-start | bytes 1310720 | tf_op jit(solution)/shard_map/all_to_all | solution.py:23
  83.4 58.6 %reduce-scatter.6.cloned.1.call-start = ((), (), s32[]{:S(2)}) async-start(), calls=%async_computation.6 | async-start | bytes 819200 | tf_op jit(solution)/shard_map/reduce_scatter | solution.py:41
  102.6 117.0 %reduce-scatter.8.cloned.1.call-start = ((), (), s32[]{:S(2)}) async-start(), calls=%async_computation.7 | async-start | bytes 696320
Sparse Core Ops, SparseCore 0:
  102.7 39.1 reduce-scatter.5
  145.3 74.2 reduce-scatter.7
where the time goes:
time: 245 us; the launch traced here: 244 us
  waiting for transfers between devices  150 us (61%)
  blocking collectives  36.7 us (15%)
  matrix products  16 us (7%)
  between operations  14.8 us (6%)
  starting transfers between devices  12 us (5%)
  local copies, waits for them, and re-layouts  8.78 us (4%)
  other arithmetic  5.74 us (2%)
    unnamed x3, waiting for transfers between devices  71.6 us
    reduce_scatter x1, waiting for transfers between devices, scatter_axes(): array = lax.psum_scatter(array, axis, scatter_dimension=dim, tiled=True)  32.7 us
    all_to_all x2, waiting for transfers between devices, sent_and_summed(): lax.all_to_all(in_blocks(array, dim, length), axis, 0, 0, tiled=True)  29.5 us
    all_to_all x1, blocking collectives, sent_to_all(): lax.all_to_all(jnp.broadcast_to(array[None], (length, *array.shape)), axi...  20.5 us
    all_to_all x1, waiting for transfers between devices, sent_to_all(): lax.all_to_all(jnp.broadcast_to(array[None], (length, *array.shape)), axi...  16.2 us
    unnamed x1, blocking collectives  16.2 us
    all_to_all x2, starting transfers between devices, sent_and_summed(): lax.all_to_all(in_blocks(array, dim, length), axis, 0, 0, tiled=True)  8.42 us
    dot_general x2, matrix products, body(): jnp.dot(context[micro_idx], w_out, preferred_element_type=jnp.float32)  7.7 us
  transfers between devices with their start and end apart: 5, of which 5 were waited for; matrix products, arithmetic and copies ran while one was open for 8% of the time, Pallas kernels for 0%

commit v1 on v0

v1 whole, which is shorter than its diff:
```python
import jax
import jax.numpy as jnp
from jax import lax
from jax.sharding import Mesh
from jax.sharding import PartitionSpec as P

DP = ("x", "z", "yh")
TENSOR = ("yl", "core")
SHAPE = (4, 16, 2, 4, 2)
BF16, F32 = jnp.bfloat16, jnp.float32


def shifted(array, axis, step):
    n = lax.axis_size(axis)
    return lax.ppermute(array, axis, [(i, (i + step) % n) for i in range(n)])


def norm_backward(hidden, gain, cot_rows):
    center = hidden - jnp.mean(hidden, axis=-1, keepdims=True)
    inverse = lax.rsqrt(jnp.mean(center * center, axis=-1, keepdims=True) + 1e-05)
    normed = center * inverse
    upstream = cot_rows.astype(F32) * gain
    result = inverse * (
        upstream
        - jnp.mean(upstream, axis=-1, keepdims=True)
        - normed * jnp.mean(upstream * normed, axis=-1, keepdims=True)
    )
    return result.astype(BF16)


def body(residual, context, w_out, gain, cotangent, slot_rows):
    micros, tokens, width = residual.shape
    heads = context.shape[-1]
    chips, cores = lax.axis_size("yl"), lax.axis_size("core")
    core, chip = lax.axis_index("core"), lax.axis_index("yl")
    rows = tokens // (chips * cores)
    share = micros * rows

    def half(array, which):
        blocks = array.reshape(micros, cores, chips, rows, array.shape[-1])
        picked = lax.dynamic_index_in_dim(blocks, which, 1, keepdims=False)
        return jnp.swapaxes(picked, 0, 1).reshape(chips * share, array.shape[-1])

    mine, theirs = half(context, core), half(context, 1 - core)
    order = slot_rows[0]

    sent = jnp.dot(theirs, w_out, preferred_element_type=F32).astype(BF16)
    received = shifted(sent, "core", 1)
    summed = jnp.dot(mine, w_out, preferred_element_type=F32) + received.astype(F32)

    def piece(array, at):
        return lax.dynamic_slice_in_dim(array, (at % chips) * share, share, 0)

    rounded = summed.astype(BF16)
    parts = [
        shifted(piece(rounded, chip + step), "yl", step) for step in range(1, chips)
    ]
    first = (core * chips + chip) * rows
    res_rows = lax.dynamic_slice_in_dim(residual, first, rows, 1).reshape(share, width)
    cot_rows = lax.dynamic_slice_in_dim(cotangent, first, rows, 1).reshape(share, width)
    hidden = res_rows.astype(F32) + piece(summed, chip)
    for part in parts:
        hidden = hidden + part.astype(F32)
    grad = norm_backward(hidden, gain, cot_rows)

    mine_grad = lax.all_gather(grad, "yl", axis=0, tiled=True)
    their_grad = shifted(mine_grad, "core", 1)

    def bucket(ctx, rows_grad):
        return lax.dot_general(
            jnp.take(ctx, order, axis=1),
            rows_grad,
            (((0,), (0,)), ((), ())),
            preferred_element_type=F32,
        )

    gradient = bucket(mine, mine_grad) + bucket(theirs, their_grad)
    slots = gradient.shape[0]
    nx, nzy = lax.axis_size("x"), lax.axis_size(("z", "yh"))
    by_x = jnp.swapaxes(gradient.astype(BF16).reshape(slots, nx, width // nx), 0, 1)
    by_x = lax.all_to_all(by_x, "x", 0, 0, tiled=True)
    plane = jnp.sum(by_x.astype(F32), axis=0).astype(BF16)
    by_zy = jnp.swapaxes(plane.reshape(slots, nzy, width // (nx * nzy)), 0, 1)
    by_zy = lax.all_to_all(by_zy, ("z", "yh"), 0, 0, tiled=True)
    reduced = jnp.sum(by_zy.astype(F32), axis=0) / lax.axis_size(DP)

    def whole(own, other):
        low = jnp.where(core == 0, own, other)
        high = jnp.where(core == 0, other, own)
        both = jnp.stack([low, high]).reshape(cores, chips, micros, rows, -1)
        return jnp.transpose(both, (2, 0, 1, 3, 4)).reshape(micros, tokens, -1)

    def back(rows_grad):
        return lax.dot_general(
            rows_grad, w_out, (((1,), (1,)), ((), ())), preferred_element_type=F32
        ).astype(BF16)

    ctx_grad = whole(back(mine_grad), back(their_grad))
    return (reduced.T[None], ctx_grad, whole(mine_grad, their_grad))


def solution(mesh):
    split = Mesh(mesh.devices.reshape(SHAPE), DP + TENSOR)
    in_specs = (
        P(None, DP, None),
        P(None, DP, TENSOR),
        P(TENSOR, None),
        P(),
        P(None, DP, None),
        P(TENSOR, None),
    )
    out_specs = (P(TENSOR, DP, None), P(None, DP, TENSOR), P(None, DP, None))
    return jax.shard_map(body, mesh=split, in_specs=in_specs, out_specs=out_specs, check_vma=False)
```

time: 245 us -> 112 us (0.46)
  waiting for transfers between devices: 150 us -> 28.9 us
  starting transfers between devices: 12 us -> 40.9 us
  blocking collectives: 36.7 us -> 17.2 us
  between operations: 14.8 us -> 0.97 us
  matrix products: 16 us -> 11.4 us
    unnamed x3 -> x0, waiting for transfers between devices: 71.6 us -> none
    reduce_scatter x1 -> x0, waiting for transfers between devices: 32.7 us -> none  [scatter_axes(): array = lax.psum_scatter(array, axis, scatter_dimension=dim, tiled=True)]
    all_to_all x3 -> x2, waiting for transfers between devices: 45.7 us -> 17.5 us  [the longest x1 16.6 us: body(): by_zy = lax.all_to_all(by_zy, ('z', 'yh'), 0, 0, tiled=True)]
    all_to_all x1 -> x0, blocking collectives: 20.5 us -> none  [sent_to_all(): lax.all_to_all(jnp.broadcast_to(array[None], (length, *array.shape)), axi...]
    all_gather x0 -> x1, blocking collectives: none -> 17.2 us  [body(): mine_grad = lax.all_gather(grad, 'yl', axis=0, tiled=True)]
    unnamed x1 -> x0, blocking collectives: 16.2 us -> none
    all_to_all x3 -> x2, starting transfers between devices: 12 us -> 26.7 us  [the longest x1 13.8 us: body(): by_x = lax.all_to_all(by_x, 'x', 0, 0, tiled=True)]
    ppermute x0 -> x5, starting transfers between devices: none -> 14.1 us  [shifted(): return lax.ppermute(array, axis, [(i, (i + step) % n) for i in range(n)])]
  transfers between devices with their start and end apart: 5 -> 7, of which waited for: 5 -> 5; matrix products, arithmetic and copies ran while one was open for 8% -> 9% of each run, Pallas kernels for 0% -> 0%
where the time goes in v1:
time: 112 us
  starting transfers between devices  40.9 us (37%)
  waiting for transfers between devices  28.9 us (26%)
  blocking collectives  17.2 us (15%)
  matrix products  11.4 us (10%)
  local copies, waits for them, and re-layouts  6.9 us (6%)
  other arithmetic  5.63 us (5%)
    all_gather x1, blocking collectives, body(): mine_grad = lax.all_gather(grad, 'yl', axis=0, tiled=True)  17.2 us
    all_to_all x1, waiting for transfers between devices, body(): by_zy = lax.all_to_all(by_zy, ('z', 'yh'), 0, 0, tiled=True)  16.6 us
    ppermute x5, starting transfers between devices, shifted(): return lax.ppermute(array, axis, [(i, (i + step) % n) for i in range(n)])  14.1 us
    all_to_all x1, starting transfers between devices, body(): by_x = lax.all_to_all(by_x, 'x', 0, 0, tiled=True)  13.8 us
    all_to_all x1, starting transfers between devices, body(): by_zy = lax.all_to_all(by_zy, ('z', 'yh'), 0, 0, tiled=True)  12.9 us
    ppermute x5, waiting for transfers between devices, shifted(): return lax.ppermute(array, axis, [(i, (i + step) % n) for i in range(n)])  11.3 us
    dot_general x2, matrix products, back(): lax.dot_general(rows_grad, w_out, (((1,), (1,)), ((), ())), preferred_ele...  4.9 us
    dot_general x1, matrix products, body(): jnp.dot(mine, w_out, preferred_element_type=F32) + received.astype(F32)  2.96 us
  transfers between devices with their start and end apart: 7, of which 5 were waited for; matrix products, arithmetic and copies ran while one was open for 9% of the time, Pallas kernels for 0%

profile of v1, /device:TPU:2, one launch (start us, length us, event | category | flops | bytes accessed | tf_op | source)
XLA Modules:
  0.0 111.8 jit_solution(16057607393611541042)
XLA Ops:
  0.6 0.8 constant_dynamic-slice_fusion.3
  1.5 0.0 copy-start.1
  1.5 2.9 %convolution_convert_fusion = bf16[64,5120]{1,0:T(8,128)(2,1)S(1)} fusion(bf16[64,384]{1,0:T(8,128)(2,1)S(1)} %bitcast.78, bf16[384,5120]{1,0:T(8,128)(2,1)} %param.10), kind=kOutput, calls=%fused_computation.2 | convolution fusion | flops 251985920 | bytes 4636672 | tf_op jit(solution)/shard_map/dot_general | solution.py:47
  4.4 1.9 %collective-permute-start = (bf16[64,5120]{1,0:T(8,128)(2,1)S(1)}, bf16[64,5120]{1,0:T(8,128)(2,1)S(1)}, u32[]{:S(2)}, u32[]{:S(2)}) collective-permute-start(bf16[64,5120]{1,0:T(8,128)(2,1)S(1)} %convolution_convert_fusion), channel_id=1, source_target_pairs={{0,1},{1,0},{2,3},{3,2},{4,5},{5,4},{6,7},{7,6},{8,9},{9,8},{10,11... | collective-permute-start | bytes 1966088 | tf_op jit(solution)/shard_map/ppermute | solution.py:15
  6.5 0.0 copy-done.1
  6.5 1.1 fusion.8
  7.5 0.9 collective-permute-done
  8.4 3.0 %fusion.25 = (bf16[64,5120]{1,0:T(8,128)(2,1)S(1)}, f32[64,5120]{1,0:T(8,128)S(1)}) fusion(bf16[64,5120]{1,0:T(8,128)(2,1)S(1)} %collective-permute-done, bf16[64,384]{1,0:T(8,128)(2,1)S(1)} %bitcast.80, bf16[384,5120]{1,0:T(8,128)(2,1)} %param.10), kind=kOutput, calls=%fused_computation.56 | convolution fusion | flops 252641280 | bytes 6602752 | tf_op jit(solution)/shard_map/dot_general | solution.py:49
  11.5 5.5 %collective-permute-start.3 = (bf16[16,5120]{1,0:T(8,128)(2,1)S(1)}, bf16[16,5120]{1,0:T(8,128)(2,1)S(1)}, u32[]{:S(2)}, u32[]{:S(2)}) collective-permute-start(bf16[16,5120]{1,0:T(8,128)(2,1)S(1)} %get-tuple-element.11), channel_id=1, source_target_pairs={{0,6},{2,0},{4,2},{6,4},{1,7},{3,1},{5,3},{7,5},{8,14},{10,8},{12,... | collective-permute-start | bytes 491528 | tf_op jit(solution)/shard_map/ppermute | solution.py:15
  17.0 1.9 %collective-permute-start.2 = (bf16[16,5120]{1,0:T(8,128)(2,1)S(1)}, bf16[16,5120]{1,0:T(8,128)(2,1)S(1)}, u32[]{:S(2)}, u32[]{:S(2)}) collective-permute-start(bf16[16,5120]{1,0:T(8,128)(2,1)S(1)} %get-tuple-element.12), channel_id=1, source_target_pairs={{0,4},{2,6},{4,0},{6,2},{1,5},{3,7},{5,1},{7,3},{8,12},{10,14},{12... | collective-permute-start | bytes 491528 | tf_op jit(solution)/shard_map/ppermute | solution.py:15
  18.9 2.9 %collective-permute-start.1 = (bf16[16,5120]{1,0:T(8,128)(2,1)S(1)}, bf16[16,5120]{1,0:T(8,128)(2,1)S(1)}, u32[]{:S(2)}, u32[]{:S(2)}) collective-permute-start(bf16[16,5120]{1,0:T(8,128)(2,1)S(1)} %get-tuple-element.10), channel_id=1, source_target_pairs={{0,2},{2,4},{4,6},{6,0},{1,3},{3,5},{5,7},{7,1},{8,10},{10,12},{12... | collective-permute-start | bytes 491528 | tf_op jit(solution)/shard_map/ppermute | solution.py:15
  21.8 0.1 div.25
  21.9 0.0 collective-permute-done.3
  21.9 10.1 %collective-permute-done.2 = bf16[16,5120]{1,0:T(8,128)(2,1)S(1)} collective-permute-done((bf16[16,5120]{1,0:T(8,128)(2,1)S(1)}, bf16[16,5120]{1,0:T(8,128)(2,1)S(1)}, u32[]{:S(2)}, u32[]{:S(2)}) %collective-permute-start.2) | collective-permute-done | bytes 163872 | tf_op jit(solution)/shard_map/ppermute | solution.py:15
  32.0 0.0 collective-permute-done.1
  32.0 1.1 %fusion.23 = (f32[16]{0:T(128)S(1)}, f32[16,5120]{1,0:T(8,128)S(1)}) fusion(bf16[16,5120]{1,0:T(8,128)(2,1)S(1)} %collective-permute-done.3, bf16[16,5120]{1,0:T(8,128)(2,1)S(1)} %collective-permute-done.2, bf16[16,5120]{1,0:T(8,128)(2,1)S(1)} %collective-permute-done.1, f32[64,5120]{1,0:T(8,128)S(1)} %get-tuple-element.7, s32[]{:T(128)S(6)} %select_n.77, ...), kind=kLoop, calls=%fused_computation.55 | loop fusion | flops 737264 | bytes 1310792 | tf_op jit(solution)/shard_map/reduce_sum | solution.py:19
  33.2 0.0 copy-start.2
  33.2 0.2 multiply_reduce_fusion
  33.4 1.1 %fusion.7 = f32[16]{0:T(128)S(1)} fusion(f32[16,5120]{1,0:T(8,128)S(1)} %get-tuple-element.5, f32[5120]{0:T(1024)S(1)} %copy-done.1, f32[16]{0:T(128)S(1)} %add_rsqrt_fusion, f32[16]{0:T(128)S(1)} %broadcast_multiply_fusion.2, bf16[2,64,5120]{2,1,0:T(8,128)(2,1)} %param.12, s32[]{:T(128)S(6)} %select_n.74), kind=kLoop, calls=%fused_computation.20 | loop fusion | flops 491504 | bytes 512196 | tf_op jit(solution)/shard_map/reduce_sum | solution.py:26
  34.6 1.1 fusion.6
  35.7 17.2 %all_gather.3 = bf16[64,5120]{1,0:T(8,128)(2,1)S(1)} all-gather(bf16[16,5120]{1,0:T(8,128)(2,1)S(1)} %fusion.6), channel_id=1, replica_groups=mesh['x'=4,'z'=16,'yh'=2,'yl'=4,'core'=2] {'yl'}, dimensions={0}, use_global_device_ids=true | all-gather | bytes 819200 | tf_op jit(solution)/shard_map/all_gather | solution.py:66
  52.9 1.9 %collective-permute-start.4 = (bf16[64,5120]{1,0:T(8,128)(2,1)S(1)}, bf16[64,5120]{1,0:T(8,128)(2,1)S(1)}, u32[]{:S(2)}, u32[]{:S(2)}) collective-permute-start(bf16[64,5120]{1,0:T(8,128)(2,1)S(1)} %all_gather.3), channel_id=1, source_target_pairs={{0,1},{1,0},{2,3},{3,2},{4,5},{5,4},{6,7},{7,6},{8,9},{9,8},{10,11... | collective-permute-start | bytes 1966088 | tf_op jit(solution)/shard_map/ppermute | solution.py:15
  54.8 0.0 copy-done.2
  54.8 0.1 copy.27
  54.9 0.1 copy.29
  55.1 0.6 gather_fusion
  55.7 0.6 gather_fusion.1
  56.3 0.3 fusion.13
  56.6 0.3 collective-permute-done.4
  56.8 0.3 fusion
  57.1 0.7 copy.38
  57.9 13.8 %all-to-all-start = ((bf16[4,32,1280]{2,1,0:T(8,128)(2,1)}), bf16[4,32,1280]{2,1,0:T(8,128)(2,1)S(1)}, u32[]{:S(2)}, u32[]{:S(2)}) async-start(bf16[4,32,1280]{2,1,0:T(8,128)(2,1)} %bitcast.72), calls=%async_computation | async-start | bytes 655360 | tf_op jit(solution)/shard_map/all_to_all | solution.py:81
  71.7 3.6 %convolution_convert_fusion.1 = bf16[64,384]{1,0:T(8,128)(2,1)S(1)} fusion(bf16[64,5120]{1,0:T(8,128)(2,1)S(1)} %collective-permute-done.4, bf16[384,5120]{1,0:T(8,128)(2,1)} %param.10), kind=kOutput, calls=%fused_computation.7 | convolution fusion | flops 251682816 | bytes 4636672 | tf_op jit(solution)/shard_map/dot_general | solution.py:94
  75.3 0.1 broadcast_select_fusion.1
  75.4 0.0 copy-done
  75.4 1.3 %broadcast_select_fusion.3 = (bf16[64,384]{1,0:T(8,128)(2,1)S(1)}, bf16[64,384]{1,0:T(8,128)(2,1)S(1)}) fusion(bf16[64,384]{1,0:T(8,128)(2,1)S(1)} %convolution_convert_fusion.1, pred[]{:T(512)S(6)} %eq.11, bf16[64,5120]{1,0:T(8,128)(2,1)S(1)} %all_gather.3, bf16[384,5120]{1,0:T(8,128)(2,1)S(1)} %copy-done), kind=kOutput, calls=%fused_computation.30 | convolution fusion | flops 251731968 | bytes 4734977 | tf_op jit(solution)/shard_map/dot_general | solution.py:94
  76.8 0.7 copy.32
  77.4 0.9 all-to-all-done
  78.4 0.4 reshape.84
  78.8 0.1 copy.31
  78.9 1.0 reshape.111
  79.9 12.9 %all-to-all-start.1 = ((bf16[32,2,640]{2,1,0:T(2,128)(2,1)}), bf16[32,2,640]{2,1,0:T(2,128)(2,1)S(1)}, u32[]{:S(2)}, u32[]{:S(2)}) async-start(bf16[32,2,640]{2,1,0:T(2,128)(2,1)} %reshape.111), calls=%async_computation.1 | async-start | bytes 163840 | tf_op jit(solution)/shard_map/all_to_all | solution.py:84
  92.8 0.1 maximum_bitcast_fusion
  93.0 1.1 %copy.33 = bf16[2,2,4,8,5120]{4,3,2,1,0:T(8,128)(2,1)} copy(bf16[2,2,4,8,5120]{4,3,0,2,1:T(8,128)(2,1)S(1)} %maximum_bitcast_fusion) | data formatting | bytes 2621440 | tf_op jit(solution)/shard_map/transpose | solution.py:91
  94.1 16.6 %all-to-all-done.1 = bf16[32,2,640]{2,1,0:T(2,128)(2,1)S(1)} async-done(((bf16[32,2,640]{2,1,0:T(2,128)(2,1)}), bf16[32,2,640]{2,1,0:T(2,128)(2,1)S(1)}, u32[]{:S(2)}, u32[]{:S(2)}) %all-to-all-start.1) | async-done | bytes 81952 | tf_op jit(solution)/shard_map/all_to_all | solution.py:84
  110.7 0.4 reshape.112
  111.2 0.1 convert_reduce_fusion
  111.2 0.6 multiply_bitcast_fusion
  (13 shorter events, 0.2 us)
Async XLA Ops:
  1.5 5.0 %copy-start.1 = (f32[5120]{0:T(1024)S(1)}, f32[5120]{0:T(1024)}, u32[]{:S(2)}) copy-start(f32[5120]{0:T(1024)} %param.11) | copy-start | bytes 61444
  4.4 4.0 %collective-permute-start = (bf16[64,5120]{1,0:T(8,128)(2,1)S(1)}, bf16[64,5120]{1,0:T(8,128)(2,1)S(1)}, u32[]{:S(2)}, u32[]{:S(2)}) collective-permute-start(bf16[64,5120]{1,0:T(8,128)(2,1)S(1)} %convolution_convert_fusion), channel_id=1, source_target_pairs={{0,1},{1,0},{2,3},{3,2},{4,5},{5,4},{6,7},{7,6},{8,9},{9,8},{10,11... | collective-permute-start | bytes 1966088 | tf_op jit(solution)/shard_map/ppermute | solution.py:15
  11.5 10.4 %collective-permute-start.3 = (bf16[16,5120]{1,0:T(8,128)(2,1)S(1)}, bf16[16,5120]{1,0:T(8,128)(2,1)S(1)}, u32[]{:S(2)}, u32[]{:S(2)}) collective-permute-start(bf16[16,5120]{1,0:T(8,128)(2,1)S(1)} %get-tuple-element.11), channel_id=1, source_target_pairs={{0,6},{2,0},{4,2},{6,4},{1,7},{3,1},{5,3},{7,5},{8,14},{10,8},{12,... | collective-permute-start | bytes 491528 | tf_op jit(solution)/shard_map/ppermute | solution.py:15
  17.0 15.1 %collective-permute-start.2 = (bf16[16,5120]{1,0:T(8,128)(2,1)S(1)}, bf16[16,5120]{1,0:T(8,128)(2,1)S(1)}, u32[]{:S(2)}, u32[]{:S(2)}) collective-permute-start(bf16[16,5120]{1,0:T(8,128)(2,1)S(1)} %get-tuple-element.12), channel_id=1, source_target_pairs={{0,4},{2,6},{4,0},{6,2},{1,5},{3,7},{5,1},{7,3},{8,12},{10,14},{12... | collective-permute-start | bytes 491528 | tf_op jit(solution)/shard_map/ppermute | solution.py:15
  18.9 13.2 %collective-permute-start.1 = (bf16[16,5120]{1,0:T(8,128)(2,1)S(1)}, bf16[16,5120]{1,0:T(8,128)(2,1)S(1)}, u32[]{:S(2)}, u32[]{:S(2)}) collective-permute-start(bf16[16,5120]{1,0:T(8,128)(2,1)S(1)} %get-tuple-element.10), channel_id=1, source_target_pairs={{0,2},{2,4},{4,6},{6,0},{1,3},{3,5},{5,7},{7,1},{8,10},{10,12},{12... | collective-permute-start | bytes 491528 | tf_op jit(solution)/shard_map/ppermute | solution.py:15
  33.2 21.6 %copy-start.2 = (s32[1,32]{1,0:T(1,128)S(1)}, s32[1,32]{1,0:T(1,128)}, u32[]{:S(2)}) copy-start(s32[1,32]{1,0:T(1,128)} %param.13) | copy-start | bytes 388
  52.9 4.0 %collective-permute-start.4 = (bf16[64,5120]{1,0:T(8,128)(2,1)S(1)}, bf16[64,5120]{1,0:T(8,128)(2,1)S(1)}, u32[]{:S(2)}, u32[]{:S(2)}) collective-permute-start(bf16[64,5120]{1,0:T(8,128)(2,1)S(1)} %all_gather.3), channel_id=1, source_target_pairs={{0,1},{1,0},{2,3},{3,2},{4,5},{5,4},{6,7},{7,6},{8,9},{9,8},{10,11... | collective-permute-start | bytes 1966088 | tf_op jit(solution)/shard_map/ppermute | solution.py:15
  57.9 20.4 %all-to-all-start = ((bf16[4,32,1280]{2,1,0:T(8,128)(2,1)}), bf16[4,32,1280]{2,1,0:T(8,128)(2,1)S(1)}, u32[]{:S(2)}, u32[]{:S(2)}) async-start(bf16[4,32,1280]{2,1,0:T(8,128)(2,1)} %bitcast.72), calls=%async_computation | async-start | bytes 655360 | tf_op jit(solution)/shard_map/all_to_all | solution.py:81
  71.7 3.7 %copy-start = (bf16[384,5120]{1,0:T(8,128)(2,1)S(1)}, bf16[384,5120]{1,0:T(8,128)(2,1)}, u32[]{:S(2)}) copy-start(bf16[384,5120]{1,0:T(8,128)(2,1)} %param.10) | copy-start | bytes 11796484
  79.9 30.8 %all-to-all-start.1 = ((bf16[32,2,640]{2,1,0:T(2,128)(2,1)}), bf16[32,2,640]{2,1,0:T(2,128)(2,1)S(1)}, u32[]{:S(2)}, u32[]{:S(2)}) async-start(bf16[32,2,640]{2,1,0:T(2,128)(2,1)} %reshape.111), calls=%async_computation.1 | async-start | bytes 163840 | tf_op jit(solution)/shard_map/all_to_all | solution.py:84
